TPU v7x, 512 devices: a 4x2x32 block of a 4x8x32 slice. The times are simulated.
512 devices in a mesh: groups: 2 (over y), tok: 32 (over z), head: 8 (over x, core).
Axes of the slice: x: 4, y: 2, z: 32, core: 2. Of those that a mesh axis runs over, the one named last changes fastest.
The devices are a block of a 4x8x32 slice.
Arguments:
- hidden: bfloat16 [20480, 8192], P(('groups', 'tok'), 'head'), parts along dimension 0, may hold values from -6 to 6
- positions: int32 [20480], P(('groups', 'tok')), parts along dimension 0, may hold values from 0 to 10239, as said below
- norm_gain: float32 [8192], P('head'), may hold values from 0.1 to 1.9
- w_key: bfloat16 [8192, 1024], P('head'), may hold values from -0.0625 to 0.0625
- w_value: bfloat16 [8192, 1024], P('head'), may hold values from -0.0625 to 0.0625
- queries: bfloat16 [512, 8192], P(('groups', 'tok'), 'head'), parts along dimension 0, may hold values from -400 to 400
- lengths: int32 [512], P(('groups', 'tok')), parts along dimension 0, may hold values from 1 to 10240
Outputs:
- attended: bfloat16 [512, 8192], P(('groups', 'tok'), 'head'), parts along dimension 0
There are 2 independent parts, one for each index of `groups`. A program takes and returns all parts, laid end to end along the dimension named above; an argument that names none is the same for every part. Nothing has to cross between parts.
Inputs may be any that keep to these rules, and one draw needn't show every extreme that they name: `positions`: each of 0 to 10239 appears once.
All inputs are finite; a program needn't handle non-finite values.
Results may differ from a plain program's by a relative error of at most 0.025.
The roundings to bfloat16 on the way count: a program that leaves them out, or rounds other values in their place, can miss the bound.
Values may be sent and summed in bfloat16 or wider, within the bound.
No kernel may reach another device: no remote copies, remote signals or barrier semaphores. Data moves between devices by JAX's collectives and lax.ppermute only.
A program may use at most 64 MiB of HBM per device.

v0:
```python
import jax
import jax.numpy as jnp
from jax import lax
from jax.sharding import PartitionSpec as P

HD = 128
QPK = 8


def copy_for_each(x, axis):
    peers = lax.axis_size(axis)
    return lax.all_to_all(jnp.broadcast_to(x[None], (peers, *x.shape)), axis, 0, 0, tiled=True)


def over_copies(x, axis):
    return copy_for_each(x, axis).max(axis=0)


def cut_along(x, dim, peers):
    before, after = (x.shape[:dim], x.shape[dim + 1 :])
    return jnp.moveaxis(x.reshape(*before, peers, -1, *after), dim, 0)


def sent_and_summed(x, axis, dim):
    peers = lax.axis_size(axis)
    pieces = lax.all_to_all(cut_along(x, dim, peers), axis, 0, 0, tiled=True)
    return jnp.sum(pieces, axis=0)


def side_by_side(arrays, axis, dim, along):
    ends, at = ([], 0)
    for a in arrays[:-1]:
        at += a.shape[along]
        ends.append(at)
    both = jnp.concatenate(arrays, axis=along)
    return tuple(jnp.split(sent_and_summed(both, axis, dim), ends, axis=along))


def rotate_columns(keys_t, positions):
    half = keys_t.shape[1] // 2
    width = keys_t.shape[1]
    freq = 500000.0 ** (-(jnp.arange(half, dtype=jnp.float32) * 2.0) / width)
    angle = positions.astype(jnp.float32)[None, :] * freq[:, None]
    cosine = jnp.cos(angle)[None]
    sine = jnp.sin(angle)[None]
    first = keys_t[:, :half]
    second = keys_t[:, half:]
    return jnp.concatenate([first * cosine - second * sine, second * cosine + first * sine], axis=1)


def project_columns(weight_rows, normed_piece):
    return lax.dot_general(
        weight_rows, normed_piece, (((0,), (1,)), ((), ())), preferred_element_type=jnp.float32
    )


def body(hidden, positions, norm_gain, w_key, w_value, queries, lengths):
    tok_rows = hidden.shape[0]
    full_width = hidden.shape[1] * lax.axis_size("head")
    kv_here = w_key.shape[1] // HD // lax.axis_size("head")
    wide = hidden.astype(jnp.float32)
    squares = lax.psum(jnp.sum(wide * wide, axis=1), "head")
    normed = (wide * lax.rsqrt(squares / full_width + 1e-05)[:, None] * norm_gain).astype(
        jnp.bfloat16
    )
    query_all, length_all = (
        lax.all_gather(queries, "tok", axis=0, tiled=True),
        lax.all_gather(lengths, "tok", axis=0, tiled=True),
    )
    stride = 2 * HD
    heads = kv_here * stride * lax.axis_size("head") // stride
    key_term = project_columns(w_key, normed).reshape(heads, HD, tok_rows)
    value_term = project_columns(w_value, normed).reshape(heads, HD, tok_rows)
    summed = lax.psum_scatter(
        jnp.stack((key_term, value_term), axis=1).reshape(heads * stride, tok_rows),
        "head",
        scatter_dimension=0,
        tiled=True,
    )
    summed = summed.reshape(kv_here, 2, HD, tok_rows)
    key_t = summed[:, 0]
    value_t = summed[:, 1]
    keys_t = rotate_columns(key_t, positions).astype(jnp.bfloat16)
    values_t = value_t.astype(jnp.bfloat16)
    row_total = query_all.shape[0]
    grouped = query_all.reshape(row_total, kv_here, QPK, HD)
    scores = jnp.einsum(
        "rjgd,jdp->jrgp", grouped, keys_t, preferred_element_type=jnp.float32
    ) * HD ** (-0.5)
    valid = positions[None, :] < length_all[:, None]
    scores = jnp.where(valid[None, :, None, :], scores, -1e30)
    top = over_copies(jnp.max(scores, axis=3), "tok")
    weights = jnp.exp(scores - top[..., None]).astype(jnp.bfloat16)
    numer = jnp.einsum("jrgp,jdp->rjgd", weights, values_t, preferred_element_type=jnp.float32)
    numer = numer.reshape(row_total, kv_here * QPK * HD)
    denom = (
        jnp.sum(weights.astype(jnp.float32), axis=3)
        .transpose(1, 0, 2)
        .reshape(row_total, kv_here * QPK)
    )
    own_rows = row_total // lax.axis_size("tok")
    numer_mine, denom_mine = side_by_side((numer, denom), "tok", 0, 1)
    result = numer_mine.reshape(own_rows, kv_here * QPK, HD) / denom_mine[..., None]
    return result.reshape(own_rows, kv_here * QPK * HD).astype(jnp.bfloat16)


def solution(mesh):
    in_specs = (
        P(("groups", "tok"), "head"),
        P(("groups", "tok")),
        P("head"),
        P("head", None),
        P("head", None),
        P(("groups", "tok"), "head"),
        P(("groups", "tok")),
    )
    out_specs = P(("groups", "tok"), "head")
    return jax.shard_map(body, mesh=mesh, in_specs=in_specs, out_specs=out_specs, check_vma=False)
```

profile of v0, /device:TPU:40, one launch (start us, length us, event | category | flops | bytes accessed | tf_op | source)
XLA Modules:
  0.0 332.2 jit_solution(14157776404545509028)
XLA Ops:
  6.5 0.0 copy-start
  6.6 0.0 reduce-scatter.2.cloned.1.call-start
  6.6 1.5 fusion.1
  8.0 15.1 %psum.7 = f32[320]{0:T(512)S(1)} all-reduce(f32[320]{0:T(512)S(1)} %fusion.1), channel_id=1, replica_groups=mesh['groups'=2,'tok'=32,'head'=8] {'head'}, use_global_device_ids=true, to_apply=%region_1.0 | all-reduce | flops 320 | bytes 2560 | tf_op jit(solution)/shard_map/psum | solution.py:62
  23.1 0.0 copy-done
  23.1 0.0 copy-start.5
  23.1 2.1 convolution_bitcast_fusion.1
  25.3 0.0 copy-start.2
  25.3 0.0 copy-start.6
  25.3 0.3 copy.31
  25.6 0.0 copy-done.5
  25.6 0.8 copy-done.2
  26.4 0.0 copy-done.6
  26.4 0.9 convolution_bitcast_fusion
  27.3 0.3 copy.32
  27.6 3.9 %pad_maximum_fusion = f32[8,2,128,320]{2,1,0,3:T(2,128)} fusion(f32[8,1,128,320]{2,1,0,3:T(1,128)S(1)} %bitcast.65, f32[8,1,128,320]{2,1,0,3:T(1,128)S(1)} %bitcast.64), kind=kLoop, calls=%fused_computation | loop fusion | flops 655360 | bytes 5242880 | tf_op jit(solution)/shard_map/stack | solution.py:75
  31.5 4.7 %reshape.189 = f32[2048,320]{0,1:T(8,128)} reshape(f32[8,2,128,320]{2,1,0,3:T(2,128)} %pad_maximum_fusion) | data formatting | bytes 5242880 | tf_op jit(solution)/shard_map/reshape | solution.py:75
  36.2 0.0 copy-start.4
  36.2 0.0 copy-start.3
  36.2 0.0 copy-start.7
  36.2 0.1 reduce-scatter.2.cloned.1.call-update
  36.3 0.6 copy-done.4
  36.9 0.0 copy-done.3
  36.9 97.5 %all_gather.7 = bf16[256,1024]{1,0:T(8,128)(2,1)S(1)} all-gather(bf16[8,1024]{1,0:T(8,128)(2,1)S(1)} %copy-done.3), channel_id=1, replica_groups=mesh['groups'=2,'tok'=32,'head'=8] {'tok'}, dimensions={0}, use_global_device_ids=true | all-gather | bytes 540672 | tf_op jit(solution)/shard_map/all_gather | solution.py:67
  134.4 0.2 copy.22
  134.6 1.3 dynamic-slice
  136.5 0.0 copy-done.7
  136.5 0.2 dynamic-update-slice
  136.8 28.9 %all-reduce = s32[256]{0:T(256)S(1)} all-reduce(s32[256]{0:T(256)S(1)} %dynamic-update-slice), channel_id=1, replica_groups=mesh['groups'=2,'tok'=32,'head'=8] {'tok'}, use_global_device_ids=true, to_apply=%add | all-reduce | flops 256 | bytes 2048
  165.7 0.1 broadcast_compare_fusion
  165.8 0.0 reduce-scatter.2.cloned.1.call-done
  165.9 1.1 reshape.190
  167.0 0.1 slice.18
  167.1 0.7 fusion.20
  167.9 2.1 fusion
  170.0 0.7 broadcast_in_dim.12
  170.7 8.6 %all-to-all-start = ((f32[32,1,256,8]{2,3,1,0:T(8,128)}), f32[32,1,256,8]{2,3,1,0:T(8,128)S(1)}, u32[]{:S(2)}, u32[]{:S(2)}) async-start(f32[32,1,256,8]{2,3,1,0:T(8,128)} %broadcast_in_dim.12), calls=%async_computation.1 | async-start | bytes 524288 | tf_op jit(solution)/shard_map/all_to_all | solution.py:12
  179.3 0.2 slice.17
  179.5 31.8 %all-to-all-done = f32[32,1,256,8]{2,3,1,0:T(8,128)S(1)} async-done(((f32[32,1,256,8]{2,3,1,0:T(8,128)}), f32[32,1,256,8]{2,3,1,0:T(8,128)S(1)}, u32[]{:S(2)}, u32[]{:S(2)}) %all-to-all-start) | async-done | bytes 262176 | tf_op jit(solution)/shard_map/all_to_all | solution.py:12
  211.4 0.0 copy-start.1
  211.4 2.4 convert_reduce_fusion
  213.8 0.1 copy-done.1
  213.9 0.8 convolution_bitcast_fusion.2
  214.7 1.3 copy.24
  216.1 1.4 concatenate.22
  217.5 0.1 copy.28
  217.6 0.1 pad_maximum_fusion.1
  217.7 106.8 %all_to_all.10 = f32[32,8,1032]{2,1,0:T(8,128)S(1)} all-to-all(f32[32,8,1032]{2,1,0:T(8,128)S(1)} %pad_maximum_fusion.1), channel_id=1, replica_groups=mesh['groups'=2,'tok'=32,'head'=8] {'tok'}, dimensions={0} | all-to-all | bytes 2113536 | tf_op jit(solution)/shard_map/all_to_all | solution.py:26
  324.5 0.1 reduce_sum.29
  324.6 0.1 copy.26
  324.7 0.7 fusion.21
  (7 shorter events, 0.1 us)
Async XLA Ops:
  6.5 16.6 %copy-start = (bf16[1024,1024]{1,0:T(8,128)(2,1)S(1)}, bf16[1024,1024]{1,0:T(8,128)(2,1)}, u32[]{:S(2)}) copy-start(bf16[1024,1024]{1,0:T(8,128)(2,1)} %param.10) | copy-start | bytes 6291460
  6.6 159.3 %reduce-scatter.2.cloned.1.call-start = ((), (), s32[]{:S(2)}) async-start(), calls=%async_computation.3 | async-start | bytes 2949120 | tf_op jit(solution)/shard_map/reduce_scatter | solution.py:74
  23.1 2.4 copy-start.5
  25.3 1.1 copy-start.2
  25.3 1.1 copy-start.6
  36.2 0.7 copy-start.4
  36.2 0.7 copy-start.3
  36.2 100.3 %copy-start.7 = (s32[8]{0:T(128)S(1)}, s32[8]{0:T(128)}, u32[]{:S(2)}) copy-start(s32[8]{0:T(128)} %param.13) | copy-start | bytes 100
  170.7 40.7 %all-to-all-start = ((f32[32,1,256,8]{2,3,1,0:T(8,128)}), f32[32,1,256,8]{2,3,1,0:T(8,128)S(1)}, u32[]{:S(2)}, u32[]{:S(2)}) async-start(f32[32,1,256,8]{2,3,1,0:T(8,128)} %broadcast_in_dim.12), calls=%async_computation.1 | async-start | bytes 524288 | tf_op jit(solution)/shard_map/all_to_all | solution.py:12
  211.4 2.5 copy-start.1
Sparse Core Ops, SparseCore 0:
  36.4 72.6 reduce-scatter.1
where the time goes:
time: 333 us; the launch traced here: 332 us
  blocking collectives  248 us (74%)
  waiting for transfers between devices  31.9 us (10%)
  between operations  14.3 us (4%)
  local copies, waits for them, and re-layouts  13.6 us (4%)
  other arithmetic  9.53 us (3%)
  starting transfers between devices  8.63 us (3%)
  matrix products  5.97 us (2%)
    all_to_all x1, blocking collectives, sent_and_summed(): pieces = lax.all_to_all(cut_along(x, dim, peers), axis, 0, 0, tiled=True)  107 us
    all_gather x1, blocking collectives, body(): lax.all_gather(queries, 'tok', axis=0, tiled=True)  97.5 us
    all_to_all x1, waiting for transfers between devices, copy_for_each(): lax.all_to_all(jnp.broadcast_to(x[None], (peers, *x.shape)), axis, 0, 0,...  31.8 us
    unnamed x1, blocking collectives  28.9 us
    psum x1, blocking collectives, body(): squares = lax.psum(jnp.sum(wide * wide, axis=1), 'head')  15.1 us
    all_to_all x1, starting transfers between devices, copy_for_each(): lax.all_to_all(jnp.broadcast_to(x[None], (peers, *x.shape)), axis, 0, 0,...  8.63 us
  transfers between devices with their start and end apart: 2, of which 1 were waited for; matrix products, arithmetic and copies ran while one was open for 1% of the time, Pallas kernels for 0%

commit v1 on v0

v1 whole, which is shorter than its diff:
```python
import functools

import jax
import jax.numpy as jnp
from jax import lax
from jax.experimental import pallas as pl
from jax.experimental.pallas import tpu as pltpu
from jax.sharding import PartitionSpec as P

HD = 128
QPK = 8
NEAR = 4
CODE = 128

F32 = jnp.float32
BF16 = jnp.bfloat16


def call(kernel, out, *args, **kw):
    return pl.pallas_call(kernel, out_shape=jax.ShapeDtypeStruct(*out), **kw)(*args)


def diagonal(n):
    return lax.broadcasted_iota(jnp.int32, (n, n), 0) == lax.broadcasted_iota(jnp.int32, (n, n), 1)


def squares_kernel(hidden, out):
    tokens = hidden.shape[0]
    wide = hidden[...].astype(F32)
    column = jnp.sum(wide * wide, axis=1, keepdims=True)
    eye = diagonal(128)
    rows = []
    for at in range(0, 1024, 128):
        if at < tokens:
            part = column[at : min(at + 128, tokens)]
            if part.shape[0] < 128:
                part = jnp.concatenate([part, jnp.zeros((128 - part.shape[0], 1), F32)], axis=0)
            rows.append(jnp.sum(jnp.where(eye, part, 0.0), axis=0, keepdims=True))
        else:
            rows.append(jnp.zeros((1, 128), F32))
    tile = jnp.concatenate(rows, axis=0)
    for peer in range(out.shape[0]):
        out[peer] = tile


def project_kernel(full_width, sums, hidden, gain, w_key, w_value, out, normed):
    tokens = hidden.shape[0]

    @pl.when(pl.program_id(0) == 0)
    def _():
        total = sums[0]
        for peer in range(1, sums.shape[0]):
            total = total + sums[peer]
        rate = lax.rsqrt(total / full_width + 1e-05)
        eye = diagonal(128)
        columns = []
        for at in range(0, tokens, 128):
            row = rate[at // 128 : at // 128 + 1]
            columns.append(jnp.sum(jnp.where(eye, row, 0.0), axis=1, keepdims=True))
        column = jnp.concatenate(columns, axis=0)[:tokens]
        normed[...] = (hidden[...].astype(F32) * column * gain[...]).astype(BF16)

    x = normed[...]
    k = jnp.dot(x, w_key[...], preferred_element_type=F32)
    v = jnp.dot(x, w_value[...], preferred_element_type=F32)
    for core in range(2):
        out[core, 0, :, :HD] = k[:, core * HD : (core + 1) * HD]
        out[core, 0, :, HD:] = v[:, core * HD : (core + 1) * HD]


def pack_kernel(parts, out):
    for x in range(out.shape[0]):
        k = parts[0, x, :, :HD] + parts[1, x, :, :HD]
        v = parts[0, x, :, HD:] + parts[1, x, :, HD:]
        high = k.astype(BF16)
        out[x, :, :HD] = high
        out[x, :, HD : 2 * HD] = (k - high.astype(F32)).astype(BF16)
        out[x, :, 2 * HD :] = v.astype(BF16)


def rotate_kernel(parts, cosine, sine, coded, out):
    tokens = parts.shape[1]
    k = jnp.zeros((tokens, HD), F32)
    v = jnp.zeros((tokens, HD), F32)
    for x in range(parts.shape[0]):
        k = k + (parts[x, :, :HD].astype(F32) + parts[x, :, HD : 2 * HD].astype(F32))
        v = v + parts[x, :, 2 * HD :].astype(F32)
    k = k * cosine[...] + pltpu.roll(k, HD // 2, 1) * sine[...]
    keys, values, where = k.astype(BF16), v.astype(BF16), coded[...]
    for peer in range(out.shape[0]):
        out[peer, :tokens, :HD] = keys
        out[peer, :tokens, HD:] = values
        out[peer, tokens:, :] = where


def attend_kernel(tokens, queries, kv, out):
    far, own = queries.shape[0], queries.shape[1]
    rows = far * own
    wide = QPK * HD
    q = []
    for h in range(QPK):
        q.append(queries[:, :, h * HD : (h + 1) * HD].astype(F32).reshape(rows, HD).astype(BF16))
    q = jnp.concatenate(q, axis=0)
    code = queries[:, :, wide:].astype(F32).reshape(rows, -1)
    length = code[:, 0:1] * CODE + code[:, 1:2]
    length = jnp.concatenate([length] * QPK, axis=0)
    scores, top = [], None
    for s in range(kv.shape[0]):
        k = kv[s, :tokens, :HD]
        x = lax.dot_general(q, k, (((1,), (1,)), ((), ())), preferred_element_type=F32) * HD**-0.5
        spare = kv[s, tokens:, :].astype(F32)
        width = spare.shape[1]
        pieces = []
        for i in range(0, tokens, width):
            take = min(width, tokens - i)
            n = i // width
            pieces.append(spare[n : n + 1, :take] * CODE + spare[8 + n : 9 + n, :take])
        place = jnp.concatenate(pieces, axis=1)
        x = jnp.where(place < length, x, -1e30)
        scores.append(x)
        here = jnp.max(x, axis=1, keepdims=True)
        top = here if top is None else jnp.maximum(top, here)
    numer = jnp.zeros((QPK * rows, HD), F32)
    denom = jnp.zeros((QPK * rows, 1), F32)
    for s in range(kv.shape[0]):
        w = jnp.exp(scores[s] - top).astype(BF16)
        denom = denom + jnp.sum(w.astype(F32), axis=1, keepdims=True)
        numer = numer + jnp.dot(w, kv[s, :tokens, HD:], preferred_element_type=F32)
    lane = lax.broadcasted_iota(jnp.int32, (rows, HD), 1)
    meta = jnp.zeros((rows, HD), F32)
    for h in range(QPK):
        part = slice(h * rows, (h + 1) * rows)
        out[:, :, h * HD : (h + 1) * HD] = numer[part].reshape(far, own, HD).astype(BF16)
        values = []
        for x, count in ((top[part], 3), (denom[part], 2)):
            for _ in range(count):
                high = x.astype(BF16).astype(F32)
                values.append(high)
                x = x - high
        for i, x in enumerate(values):
            meta = jnp.where(lane == 5 * h + i, x, meta)
    out[:, :, wide:] = meta.reshape(far, own, HD).astype(BF16)


def merge_kernel(parts, out):
    wide = QPK * HD
    meta = parts[:, :, wide:].astype(F32)
    for h in range(QPK):
        at = 5 * h
        top = meta[:, :, at : at + 1] + meta[:, :, at + 1 : at + 2] + meta[:, :, at + 2 : at + 3]
        denom = meta[:, :, at + 3 : at + 4] + meta[:, :, at + 4 : at + 5]
        scale = jnp.exp(top - jnp.max(top, axis=0, keepdims=True))
        numer = jnp.sum(parts[:, :, h * HD : (h + 1) * HD].astype(F32) * scale, axis=0)
        out[:, h * HD : (h + 1) * HD] = (numer / jnp.sum(denom * scale, axis=0)).astype(BF16)


def coded_pair(x):
    return (x // CODE).astype(BF16), (x % CODE).astype(BF16)


def body(hidden, positions, norm_gain, w_key, w_value, queries, lengths):
    tokens, width = hidden.shape
    heads, toks = lax.axis_size("head"), lax.axis_size("tok")
    chips = heads // 2
    far = toks // NEAR
    own = queries.shape[0]
    cores = [[2 * x, 2 * x + 1] for x in range(chips)]
    row = [[2 * x + c for x in range(chips)] for c in range(2)]
    near = [[NEAR * b + i for i in range(NEAR)] for b in range(far)]
    stride = [[NEAR * b + i for b in range(far)] for i in range(NEAR)]

    high, low = coded_pair(lengths)
    extra = jnp.pad(jnp.stack([high, low], axis=1), ((0, 0), (0, HD - 2)))
    asked = jnp.concatenate([queries, extra], axis=1)
    asked = jnp.broadcast_to(asked[None], (far, *asked.shape))
    asked = lax.all_to_all(asked, "tok", 0, 0, axis_index_groups=stride, tiled=True)

    sums = call(squares_kernel, ((heads, 8, 128), F32), hidden)
    sums = lax.all_to_all(sums, "head", 0, 0, tiled=True)

    half = HD // 2
    freq = 500000.0 ** (-(jnp.arange(half, dtype=F32) * 2.0) / HD)
    angle = positions.astype(F32)[:, None] * freq[None, :]
    cosine, sine = jnp.cos(angle), jnp.sin(angle)
    cosine = jnp.concatenate([cosine, cosine], axis=1)
    sine = jnp.concatenate([-sine, sine], axis=1)
    spare = 8 * 2 * HD - tokens
    coded = jnp.concatenate([jnp.pad(x, (0, spare)).reshape(8, 2 * HD) for x in coded_pair(positions)])

    columns = w_key.shape[1] // chips
    block = lambda *shape: pl.BlockSpec(shape, lambda i: (0,) * len(shape))
    strip = pl.BlockSpec((width, columns), lambda i: (0, i))
    parts = call(
        functools.partial(project_kernel, width * heads),
        ((2, chips, tokens, 2 * HD), F32),
        sums,
        hidden,
        norm_gain[None],
        w_key,
        w_value,
        grid=(chips,),
        in_specs=[block(*sums.shape), block(tokens, width), block(1, width), strip, strip],
        out_specs=pl.BlockSpec((2, 1, tokens, 2 * HD), lambda i: (0, i, 0, 0)),
        scratch_shapes=[pltpu.VMEM((tokens, width), BF16)],
    )
    parts = lax.all_to_all(parts, "head", 0, 0, axis_index_groups=cores, tiled=True)
    parts = call(pack_kernel, ((chips, tokens, 3 * HD), BF16), parts)
    parts = lax.all_to_all(parts, "head", 0, 0, axis_index_groups=row, tiled=True)
    kv = call(rotate_kernel, ((NEAR, tokens + 16, 2 * HD), BF16), parts, cosine, sine, coded)
    kv = lax.all_to_all(kv, "tok", 0, 0, axis_index_groups=near, tiled=True)
    part = call(
        functools.partial(attend_kernel, tokens), ((far, own, QPK * HD + HD), BF16), asked, kv
    )
    part = lax.all_to_all(part, "tok", 0, 0, axis_index_groups=stride, tiled=True)
    return call(merge_kernel, ((own, QPK * HD), BF16), part)


def solution(mesh):
    in_specs = (
        P(("groups", "tok"), "head"),
        P(("groups", "tok")),
        P("head"),
        P("head", None),
        P("head", None),
        P(("groups", "tok"), "head"),
        P(("groups", "tok")),
    )
    out_specs = P(("groups", "tok"), "head")
    return jax.shard_map(body, mesh=mesh, in_specs=in_specs, out_specs=out_specs, check_vma=False)
```

time: 333 us -> 186 us (0.56)
  blocking collectives: 248 us -> 74.9 us
  starting transfers between devices: 8.63 us -> 47 us
  Pallas kernels: 0 us -> 18.5 us
  between operations: 14.3 us -> 0.09 us
  local copies, waits for them, and re-layouts: 13.6 us -> 0.84 us
  waiting for transfers between devices: 31.9 us -> 42.1 us
  other arithmetic: 9.53 us -> 2.19 us
  matrix products: 5.97 us -> 0 us
    all_gather x1 -> x0, blocking collectives: 97.5 us -> none  [body(): lax.all_gather(queries, 'tok', axis=0, tiled=True)]
    all_to_all x1 -> x2, starting transfers between devices: 8.63 us -> 47 us  [the longest x1 43.4 us: body(): lax.all_to_all(asked, 'tok', 0, 0, axis_index_groups=stride, tiled=True)]
    all_to_all x1 -> x4, blocking collectives: 107 us -> 74.9 us  [the longest x1 34.1 us: body(): lax.all_to_all(part, 'tok', 0, 0, axis_index_groups=stride, tiled=True)]
    unnamed x1 -> x0, blocking collectives: 28.9 us -> none
    pallas_call x0 -> x6, Pallas kernels: none -> 18.5 us  [call(): pl.pallas_call(kernel, out_shape=jax.ShapeDtypeStruct(*out), **kw)(*args)]
    psum x1 -> x0, blocking collectives: 15.1 us -> none  [body(): squares = lax.psum(jnp.sum(wide * wide, axis=1), 'head')]
    all_to_all x1 -> x2, waiting for transfers between devices: 31.8 us -> 42.1 us  [the longest x1 27.3 us: body(): lax.all_to_all(asked, 'tok', 0, 0, axis_index_groups=stride, tiled=True)]
    dot_general x4 -> x0, matrix products: 5.97 us -> none  [the longest x2 3.04 us: project_columns(): lax.dot_general(weight_rows, normed_piece, (((0,), (1,)), ((), ())), pref...]
  transfers between devices with their start and end apart: 2 -> 2, of which waited for: 1 -> 2; matrix products, arithmetic and copies ran while one was open for 1% -> 1% of each run, Pallas kernels for 0% -> 1%
where the time goes in v1:
time: 186 us
  blocking collectives  74.9 us (40%)
  starting transfers between devices  47 us (25%)
  waiting for transfers between devices  42.1 us (23%)
  Pallas kernels  18.5 us (10%)
  other arithmetic  2.19 us (1%)
    all_to_all x1, starting transfers between devices, body(): lax.all_to_all(asked, 'tok', 0, 0, axis_index_groups=stride, tiled=True)  43.4 us
    all_to_all x1, blocking collectives, body(): lax.all_to_all(part, 'tok', 0, 0, axis_index_groups=stride, tiled=True)  34.1 us
    all_to_all x1, waiting for transfers between devices, body(): lax.all_to_all(asked, 'tok', 0, 0, axis_index_groups=stride, tiled=True)  27.3 us
    all_to_all x1, blocking collectives, body(): kv = lax.all_to_all(kv, 'tok', 0, 0, axis_index_groups=near, tiled=True)  21.3 us
    pallas_call x6, Pallas kernels, call(): pl.pallas_call(kernel, out_shape=jax.ShapeDtypeStruct(*out), **kw)(*args)  18.5 us
    all_to_all x1, waiting for transfers between devices, body(): lax.all_to_all(parts, 'head', 0, 0, axis_index_groups=row, tiled=True)  14.7 us
    all_to_all x1, blocking collectives, body(): sums = lax.all_to_all(sums, 'head', 0, 0, tiled=True)  10.1 us
    all_to_all x1, blocking collectives, body(): lax.all_to_all(parts, 'head', 0, 0, axis_index_groups=cores, tiled=True)  9.39 us
  transfers between devices with their start and end apart: 2, of which 2 were waited for; matrix products, arithmetic and copies ran while one was open for 1% of the time, Pallas kernels for 1%

profile of v1, /device:TPU:40, one launch (start us, length us, event | category | flops | bytes accessed | tf_op | source)
XLA Modules:
  0.0 185.7 jit_solution(16385208739926829851)
XLA Ops:
  0.0 2.0 %shard_map.73 = f32[8,8,128]{2,1,0:T(8,128)} custom-call(bf16[320,1024]{1,0:T(8,128)(2,1)} %hidden.3), custom_call_target="tpu_custom_call" | custom-call | tf_op jit(solution)/shard_map/pallas_call | solution.py:20
  2.0 10.1 %all_to_all.30.sums = f32[8,8,128]{2,1,0:T(8,128)} all-to-all(f32[8,8,128]{2,1,0:T(8,128)} %shard_map.73), channel_id=1, replica_groups=mesh['groups'=2,'tok'=32,'head'=8] {'head'}, dimensions={0} | all-to-all | bytes 65536 | tf_op jit(solution)/shard_map/all_to_all | solution.py:179
  12.1 5.8 %shard_map.74 = f32[2,4,320,256]{3,2,1,0:T(8,128)} custom-call(f32[8,8,128]{2,1,0:T(8,128)} %all_to_all.30.sums, bf16[320,1024]{1,0:T(8,128)(2,1)} %hidden.3, f32[1,1024]{1,0:T(1,128)} %bitcast.5, bf16[1024,1024]{1,0:T(8,128)(2,1)} %w_key.1, bf16[1024,1024]{1,0:T(8,128)(2,1)} %w_value.1), custom_call_target="tpu_custom_call" | custom-call | tf_op jit(solution)/shard_map/pallas_call | solution.py:20
  17.9 9.4 %all_to_all.31.parts = f32[2,4,320,256]{3,2,1,0:T(8,128)} all-to-all(f32[2,4,320,256]{3,2,1,0:T(8,128)} %shard_map.74), channel_id=1, replica_groups={{0,1},{2,3},{4,5},{6,7},{8,9},{10,11},{12,13},{14,15},{16,17},{18,19},{..., dimensions={0} | all-to-all | bytes 5242880 | tf_op jit(solution)/shard_map/all_to_all | solution.py:206
  27.3 0.0 copy-start.4
  27.3 0.0 copy-start.2
  27.3 0.0 copy-start.3
  27.3 2.9 %shard_map.75 = bf16[4,320,384]{2,1,0:T(8,128)(2,1)} custom-call(f32[2,4,320,256]{3,2,1,0:T(8,128)} %all_to_all.31.parts), custom_call_target="tpu_custom_call" | custom-call | tf_op jit(solution)/shard_map/pallas_call | solution.py:20
  30.2 3.6 %all-to-all-start.3 = ((bf16[4,320,384]{2,1,0:T(8,128)(2,1)}), bf16[4,320,384]{2,1,0:T(8,128)(2,1)S(1)}, u32[]{:S(2)}, u32[]{:S(2)}) async-start(bf16[4,320,384]{2,1,0:T(8,128)(2,1)} %shard_map.75), calls=%async_computation.3 | async-start | bytes 1966080 | tf_op jit(solution)/shard_map/all_to_all | solution.py:208
  33.8 0.0 copy-done.4
  33.9 0.1 copy.9
  34.0 0.0 copy-done.2
  34.0 14.7 %all-to-all-done.3.parts = bf16[4,320,384]{2,1,0:T(8,128)(2,1)S(1)} async-done(((bf16[4,320,384]{2,1,0:T(8,128)(2,1)}), bf16[4,320,384]{2,1,0:T(8,128)(2,1)S(1)}, u32[]{:S(2)}, u32[]{:S(2)}) %all-to-all-start.3) | async-done | bytes 983072 | tf_op jit(solution)/shard_map/all_to_all | solution.py:208
  48.7 0.0 copy-start
  48.7 0.7 broadcast_in_dim.4
  49.4 43.4 %all-to-all-start = ((bf16[8,8,1152]{2,1,0:T(8,128)(2,1)}), bf16[8,8,1152]{2,1,0:T(8,128)(2,1)S(1)}, u32[]{:S(2)}, u32[]{:S(2)}) async-start(bf16[8,8,1152]{2,1,0:T(8,128)(2,1)} %broadcast_in_dim.4), calls=%async_computation | async-start | bytes 294912 | tf_op jit(solution)/shard_map/all_to_all | solution.py:176
  92.8 0.0 copy-done.3
  92.9 0.6 pad_maximum_fusion.2.coded
  93.5 0.6 fusion
  94.2 0.9 pad_maximum_fusion
  95.1 0.0 copy-done
  95.1 2.4 %shard_map.76 = bf16[4,336,256]{2,1,0:T(8,128)(2,1)} custom-call(bf16[4,320,384]{2,1,0:T(8,128)(2,1)} %copy-done, f32[320,128]{1,0:T(8,128)} %get-tuple-element.13.cosine, f32[320,128]{1,0:T(8,128)} %get-tuple-element.14.sine, bf16[16,256]{1,0:T(8,128)(2,1)} %pad_maximum_fusion.2.coded), custom_call_target="tpu_custom_call" | custom-call | tf_op jit(solution)/shard_map/pallas_call | solution.py:20
  97.5 27.3 %all-to-all-done.queries = bf16[8,8,1152]{2,1,0:T(8,128)(2,1)S(1)} async-done(((bf16[8,8,1152]{2,1,0:T(8,128)(2,1)}), bf16[8,8,1152]{2,1,0:T(8,128)(2,1)S(1)}, u32[]{:S(2)}, u32[]{:S(2)}) %all-to-all-start) | async-done | bytes 147488 | tf_op jit(solution)/shard_map/all_to_all | solution.py:176
  124.8 0.0 copy-start.1
  124.8 21.3 %all_to_all.32.kv = bf16[4,336,256]{2,1,0:T(8,128)(2,1)} all-to-all(bf16[4,336,256]{2,1,0:T(8,128)(2,1)} %shard_map.76), channel_id=1, replica_groups={{0,8,16,24},{32,40,48,56},{64,72,80,88},{96,104,112,120},{128,136,144,1..., dimensions={0} | all-to-all | bytes 1376256 | tf_op jit(solution)/shard_map/all_to_all | solution.py:210
  146.1 0.0 copy-done.1
  146.1 3.6 %shard_map.77 = bf16[8,8,1152]{2,1,0:T(8,128)(2,1)} custom-call(bf16[8,8,1152]{2,1,0:T(8,128)(2,1)} %copy-done.1, bf16[4,336,256]{2,1,0:T(8,128)(2,1)} %all_to_all.32.kv), custom_call_target="tpu_custom_call" | custom-call | tf_op jit(solution)/shard_map/pallas_call | solution.py:20
  149.7 34.1 %all_to_all.33.parts = bf16[8,8,1152]{2,1,0:T(8,128)(2,1)} all-to-all(bf16[8,8,1152]{2,1,0:T(8,128)(2,1)} %shard_map.77), channel_id=1, replica_groups={{0,32,64,96,128,160,192,224},{8,40,72,104,136,168,200,232},{16,48,80,11..., dimensions={0} | all-to-all | bytes 294912 | tf_op jit(solution)/shard_map/all_to_all | solution.py:214
  183.8 1.9 %shard_map.78 = bf16[8,1024]{1,0:T(8,128)(2,1)} custom-call(bf16[8,8,1152]{2,1,0:T(8,128)(2,1)} %all_to_all.33.parts), custom_call_target="tpu_custom_call" | custom-call | tf_op jit(solution)/shard_map/pallas_call | solution.py:20
  (9 shorter events, 0.1 us)
Async XLA Ops:
  27.3 6.6 %copy-start.4 = (s32[8]{0:T(128)S(1)}, s32[8]{0:T(128)}, u32[]{:S(2)}) copy-start(s32[8]{0:T(128)} %param.13) | copy-start | bytes 100
  27.3 6.7 %copy-start.2 = (bf16[8,1024]{1,0:T(8,128)(2,1)S(1)}, bf16[8,1024]{1,0:T(8,128)(2,1)}, u32[]{:S(2)}) copy-start(bf16[8,1024]{1,0:T(8,128)(2,1)} %param.12) | copy-start | bytes 49156
  27.3 65.6 %copy-start.3 = (s32[320]{0:T(512)S(1)}, s32[320]{0:T(512)}, u32[]{:S(2)}) copy-start(s32[320]{0:T(512)} %param.8) | copy-start | bytes 3844
  30.2 18.5 %all-to-all-start.3 = ((bf16[4,320,384]{2,1,0:T(8,128)(2,1)}), bf16[4,320,384]{2,1,0:T(8,128)(2,1)S(1)}, u32[]{:S(2)}, u32[]{:S(2)}) async-start(bf16[4,320,384]{2,1,0:T(8,128)(2,1)} %shard_map.75), calls=%async_computation.3 | async-start | bytes 1966080 | tf_op jit(solution)/shard_map/all_to_all | solution.py:208
  48.7 46.4 %copy-start = (bf16[4,320,384]{2,1,0:T(8,128)(2,1)}, bf16[4,320,384]{2,1,0:T(8,128)(2,1)S(1)}, u32[]{:S(2)}) copy-start(bf16[4,320,384]{2,1,0:T(8,128)(2,1)S(1)} %all-to-all-done.3.parts) | copy-start | bytes 2949124
  49.4 75.4 %all-to-all-start = ((bf16[8,8,1152]{2,1,0:T(8,128)(2,1)}), bf16[8,8,1152]{2,1,0:T(8,128)(2,1)S(1)}, u32[]{:S(2)}, u32[]{:S(2)}) async-start(bf16[8,8,1152]{2,1,0:T(8,128)(2,1)} %broadcast_in_dim.4), calls=%async_computation | async-start | bytes 294912 | tf_op jit(solution)/shard_map/all_to_all | solution.py:176
  124.8 21.3 %copy-start.1 = (bf16[8,8,1152]{2,1,0:T(8,128)(2,1)}, bf16[8,8,1152]{2,1,0:T(8,128)(2,1)S(1)}, u32[]{:S(2)}) copy-start(bf16[8,8,1152]{2,1,0:T(8,128)(2,1)S(1)} %all-to-all-done.queries) | copy-start | bytes 442372
